TPU v7x, 32 devices: a whole 2x2x4 slice. The times are simulated.
32 devices in a mesh: rep: 4 (over x, core), fsdp: 8 (over z, y).
Axes of the slice: x: 2, y: 2, z: 4, core: 2. Of those that a mesh axis runs over, the one named last changes fastest.
Arguments:
- tokens: bfloat16 [32768, 1024], P(('rep', 'fsdp')), may hold values from -6 to 6
- cotangent: bfloat16 [32768, 1024], P(('rep', 'fsdp')), may hold values from -6 to 6
- segment_ids: int32 [32, 1024], P(('rep', 'fsdp')), may hold values from 0 to 15, never falling along the last dimension, each value on 1 to 512 neighbouring positions
- attention_weight: float32 [4, 1024, 1024], P(None, 'fsdp'), may hold values from -0.375 to 0.375
- attention_momentum: float32 [4, 1024, 1024], P(None, 'fsdp'), may hold values from -0.1875 to 0.1875
- attention_first: float32 [4, 4, 1024, 1024], P('rep', None, 'fsdp'), may hold values from -112 to 112
- attention_second: float32 [4, 4, 1024, 1024], P('rep', None, 'fsdp'), may hold values from 54.8864 to 876.544
- expand_weight: float32 [1024, 4096], P('fsdp'), may hold values from -0.1875 to 0.1875
- expand_momentum: float32 [1024, 4096], P('fsdp'), may hold values from -0.1875 to 0.1875
- expand_first: float32 [4, 1024, 4096], P('rep', 'fsdp'), may hold values from -128 to 128
- expand_second: float32 [4, 1024, 4096], P('rep', 'fsdp'), may hold values from 85.1968 to 1368.064
- contract_weight: float32 [4096, 1024], P('fsdp'), may hold values from -0.09375 to 0.09375
- contract_momentum: float32 [4096, 1024], P('fsdp'), may hold values from -0.09375 to 0.09375
- contract_first: float32 [4, 4096, 1024], P('rep', 'fsdp'), may hold values from -256 to 256
- contract_second: float32 [4, 4096, 1024], P('rep', 'fsdp'), may hold values from 341.6064 to 5464.064
- vectors: float32 [12, 1024], P(None, 'fsdp'), may hold values from -0.6 to 1.4
- vectors_momentum: float32 [12, 1024], P(None, 'fsdp'), may hold values from -1.25 to 1.25
- vectors_first: float32 [4, 12, 1024], P('rep', None, 'fsdp'), may hold values from -448 to 448
- vectors_second: float32 [4, 12, 1024], P('rep', None, 'fsdp'), may hold values from 876.544 to 14008.32
Outputs:
- layer_output: bfloat16 [32768, 1024], P(('rep', 'fsdp'))
- input_grad: bfloat16 [32768, 1024], P(('rep', 'fsdp'))
- attention_first_new: float32 [4, 4, 1024, 1024], P('rep', None, 'fsdp')
- attention_second_new: float32 [4, 4, 1024, 1024], P('rep', None, 'fsdp')
- outer_attention: float32 [3, 4, 1024, 1024], P(None, None, 'fsdp')
- copy_attention: bfloat16 [4, 1024, 1024], P(None, 'fsdp')
- expand_first_new: float32 [4, 1024, 4096], P('rep', 'fsdp')
- expand_second_new: float32 [4, 1024, 4096], P('rep', 'fsdp')
- outer_expand: float32 [3, 1024, 4096], P(None, 'fsdp')
- copy_expand: bfloat16 [1024, 4096], P('fsdp')
- contract_first_new: float32 [4, 4096, 1024], P('rep', 'fsdp')
- contract_second_new: float32 [4, 4096, 1024], P('rep', 'fsdp')
- outer_contract: float32 [3, 4096, 1024], P(None, 'fsdp')
- copy_contract: bfloat16 [4096, 1024], P('fsdp')
- vectors_first_new: float32 [4, 12, 1024], P('rep', None, 'fsdp')
- vectors_second_new: float32 [4, 12, 1024], P('rep', None, 'fsdp')
- outer_vectors: float32 [3, 12, 1024], P(None, None, 'fsdp')
- copy_vectors: bfloat16 [12, 1024], P(None, 'fsdp')
Inputs may be any that keep to these rules, and one draw needn't show every extreme that they name: `segment_ids`: within a row the numbers never fall; a run of equal numbers is one document, and tokens attend only within their document.
All inputs are finite; a program needn't handle non-finite values.
Results may differ from a plain program's by a relative error of at most 0.012.
The roundings to bfloat16 on the way count: a program that leaves them out, or rounds other values in their place, can miss the bound.
Values may be sent and summed in bfloat16 or wider, within the bound.
A program may use at most 448 MiB of HBM per device.

v0:
```python
from functools import partial
import jax
import jax.numpy as jnp
from jax import lax
from jax.sharding import PartitionSpec as P

D = 1024
H = 16
HD = 64
FF = 4096
LEN = 1024
SEQ_DEV = 1
ADAM_STEP = 4
TOK_DEV = 1024


def norm_forward(values_in, gain_row, shift_row):
    center = values_in - jnp.mean(values_in, axis=-1, keepdims=True)
    inv_scale = lax.rsqrt(jnp.mean(center * center, axis=-1, keepdims=True) + 1e-05)
    normed = center * inv_scale
    return (normed * gain_row + shift_row, normed, inv_scale)


def norm_backward(grad_out, normed, inv_scale, gain_row):
    grad_gain = jnp.sum(grad_out * normed, axis=0)
    grad_shift = jnp.sum(grad_out, axis=0)
    scaled_grad = grad_out * gain_row
    grad_value = inv_scale * (
        scaled_grad
        - jnp.mean(scaled_grad, axis=-1, keepdims=True)
        - normed * jnp.mean(scaled_grad * normed, axis=-1, keepdims=True)
    )
    return (grad_value, grad_gain, grad_shift)


def product_over(left, right):
    return lax.dot_general(
        left, right, (((0,), (0,)), ((), ())), preferred_element_type=jnp.float32
    )


def product_back(left, right):
    return lax.dot_general(
        left, right, (((1,), (1,)), ((), ())), preferred_element_type=jnp.float32
    )


def block_scores(query_block, key_block, row_segments, all_segments):
    scores = jnp.einsum("qhd,khd->hqk", query_block, key_block, preferred_element_type=jnp.float32)
    same_doc = row_segments[:, None] == all_segments[None, :]
    return jnp.where(same_doc[None], scores, -1e30)


def inner_step(weight, gradient, first_moment, second_moment, learn_rate, weight_decay):
    first_new = 0.5 * first_moment + 0.5 * gradient
    second_new = 0.75 * second_moment + 0.25 * gradient * gradient
    update_dir = (
        first_new
        / (1.0 - 0.5**ADAM_STEP)
        / (jnp.sqrt(second_new / (1.0 - 0.75**ADAM_STEP)) + 1e-08)
    )
    return (weight - learn_rate * (update_dir + weight_decay * weight), first_new, second_new)


def per_device(
    tokens,
    cotangent,
    segment_ids,
    attention_weight,
    attention_momentum,
    attention_first,
    attention_second,
    expand_weight,
    expand_momentum,
    expand_first,
    expand_second,
    contract_weight,
    contract_momentum,
    contract_first,
    contract_second,
    vectors,
    vectors_momentum,
    vectors_first,
    vectors_second,
):
    attn_full, vector_full = (
        lax.all_gather(attention_weight.astype(jnp.bfloat16), "fsdp", axis=1, tiled=True),
        lax.all_gather(vectors.astype(jnp.bfloat16), "fsdp", axis=1, tiled=True),
    )
    vector_rows = vector_full.astype(jnp.float32)
    gain_one, gain_two, shift_one, shift_two = (
        vector_rows[0],
        vector_rows[1],
        vector_rows[2],
        vector_rows[3],
    )
    bias_query, bias_value, bias_mixed, bias_down = (
        vector_rows[4],
        vector_rows[5],
        vector_rows[6],
        vector_rows[7],
    )
    bias_up = vector_rows[8:].reshape(FF)
    projected = jnp.einsum("td,nde->nte", tokens, attn_full[:3], preferred_element_type=jnp.float32)
    query_all = ((projected[0] + bias_query) * 0.125).astype(jnp.bfloat16)
    key_all = projected[1].astype(jnp.bfloat16)
    value_all = (projected[2] + bias_value).astype(jnp.bfloat16)
    query_heads = query_all.reshape(SEQ_DEV, LEN, H, HD)
    key_heads = key_all.reshape(SEQ_DEV, LEN, H, HD)
    value_heads = value_all.reshape(SEQ_DEV, LEN, H, HD)
    block_rows = min(512, LEN)
    head_group = min(8, H)
    context_rows = []
    log_sums = []
    seq_index = 0
    for row_start in range(0, LEN, block_rows):
        block_pieces = []
        for head_start in range(0, H, head_group):
            head_part = slice(head_start, head_start + head_group)
            scores = block_scores(
                query_heads[seq_index, row_start : row_start + block_rows, head_part],
                key_heads[seq_index, :, head_part],
                segment_ids[seq_index, row_start : row_start + block_rows],
                segment_ids[seq_index],
            )
            row_max = jnp.max(scores, axis=-1, keepdims=True)
            exp_score = jnp.exp(scores - row_max)
            row_total = jnp.sum(exp_score, axis=-1, keepdims=True)
            probability = (exp_score / row_total).astype(jnp.bfloat16)
            block_pieces.append(
                jnp.einsum(
                    "hqk,khd->qhd",
                    probability,
                    value_heads[seq_index, :, head_part],
                    preferred_element_type=jnp.float32,
                )
            )
            log_sums.append(row_max + jnp.log(row_total))
        context_rows.append(jnp.concatenate(block_pieces, axis=1))
    mixed = jnp.concatenate(context_rows, axis=0).reshape(TOK_DEV, D).astype(jnp.bfloat16)
    attn_out = jnp.dot(mixed, attn_full[3], preferred_element_type=jnp.float32) + bias_mixed
    hidden, normed_one, scale_one = norm_forward(
        tokens.astype(jnp.float32) + attn_out, gain_one, shift_one
    )
    hidden_low = hidden.astype(jnp.bfloat16)
    ffn_expand, ffn_contract = (
        lax.all_gather(expand_weight.astype(jnp.bfloat16), "fsdp", axis=0, tiled=True),
        lax.all_gather(contract_weight.astype(jnp.bfloat16), "fsdp", axis=0, tiled=True),
    )
    pre_act = jnp.dot(hidden_low, ffn_expand, preferred_element_type=jnp.float32) + bias_up
    activated = jax.nn.gelu(pre_act, approximate=False).astype(jnp.bfloat16)
    branch = jnp.dot(activated, ffn_contract, preferred_element_type=jnp.float32) + bias_down
    layer_output, normed_two, scale_two = norm_forward(hidden + branch, gain_two, shift_two)
    grad_sum, grad_gain_two, grad_shift_two = norm_backward(
        cotangent.astype(jnp.float32), normed_two, scale_two, gain_two
    )
    grad_branch = grad_sum.astype(jnp.bfloat16)
    grad_act = product_back(grad_branch, ffn_contract)
    unused_value, gelu_pull = jax.vjp(partial(jax.nn.gelu, approximate=False), pre_act)
    grad_pre_low = gelu_pull(grad_act)[0].astype(jnp.bfloat16)
    grad_hidden = grad_sum + product_back(grad_pre_low, ffn_expand)
    contract_full = product_over(activated, grad_branch)
    expand_full = product_over(hidden_low, grad_pre_low)
    grad_expand, grad_contract = (
        lax.psum_scatter(expand_full, "fsdp", scatter_dimension=0, tiled=True),
        lax.psum_scatter(contract_full, "fsdp", scatter_dimension=0, tiled=True),
    )
    grad_resid, grad_gain_one, grad_shift_one = norm_backward(
        grad_hidden, normed_one, scale_one, gain_one
    )
    grad_attn_out = grad_resid.astype(jnp.bfloat16)
    grad_bias_mixed = jnp.sum(grad_attn_out.astype(jnp.float32), axis=0)
    grad_output_proj = product_over(mixed, grad_attn_out)
    grad_mixed = product_back(grad_attn_out, attn_full[3]).astype(jnp.bfloat16)
    grad_context = grad_mixed.reshape(SEQ_DEV, LEN, H, HD)
    query_grads = []
    lse_index = 0
    seq_index = 0
    key_totals = [
        jnp.zeros((LEN, head_group, HD), jnp.float32) for head_start in range(0, H, head_group)
    ]
    value_totals = [
        jnp.zeros((LEN, head_group, HD), jnp.float32) for head_start in range(0, H, head_group)
    ]
    for row_start in range(0, LEN, block_rows):
        block_pieces = []
        for group_index, head_start in enumerate(range(0, H, head_group)):
            head_part = slice(head_start, head_start + head_group)
            query_block = query_heads[seq_index, row_start : row_start + block_rows, head_part]
            key_block = key_heads[seq_index, :, head_part]
            value_block = value_heads[seq_index, :, head_part]
            ctx_grad = grad_context[seq_index, row_start : row_start + block_rows, head_part]
            scores = block_scores(
                query_block,
                key_block,
                segment_ids[seq_index, row_start : row_start + block_rows],
                segment_ids[seq_index],
            )
            probability = jnp.exp(scores - log_sums[lse_index])
            lse_index = lse_index + 1
            value_totals[group_index] = value_totals[group_index] + jnp.einsum(
                "hqk,qhd->khd",
                probability.astype(jnp.bfloat16),
                ctx_grad,
                preferred_element_type=jnp.float32,
            )
            prob_grad = jnp.einsum(
                "qhd,khd->hqk", ctx_grad, value_block, preferred_element_type=jnp.float32
            )
            row_dot = jnp.sum(probability * prob_grad, axis=-1, keepdims=True)
            score_grad = (probability * (prob_grad - row_dot)).astype(jnp.bfloat16)
            block_pieces.append(
                jnp.einsum(
                    "hqk,khd->qhd", score_grad, key_block, preferred_element_type=jnp.float32
                ).astype(jnp.bfloat16)
            )
            key_totals[group_index] = key_totals[group_index] + jnp.einsum(
                "hqk,qhd->khd", score_grad, query_block, preferred_element_type=jnp.float32
            )
        query_grads.append(jnp.concatenate(block_pieces, axis=1))
    key_grads = jnp.concatenate(
        [key_total.astype(jnp.bfloat16) for key_total in key_totals], axis=1
    )
    value_grads = jnp.concatenate(
        [value_total.astype(jnp.bfloat16) for value_total in value_totals], axis=1
    )
    grad_query = jnp.concatenate(query_grads, axis=0).reshape(TOK_DEV, D) * 0.125
    grad_keys = key_grads.reshape(TOK_DEV, D)
    grad_values = value_grads.reshape(TOK_DEV, D)
    stacked_grads = jnp.stack([grad_query, grad_keys, grad_values])
    grad_qkv = jnp.einsum("td,nte->nde", tokens, stacked_grads, preferred_element_type=jnp.float32)
    input_grad = (
        grad_resid
        + jnp.einsum(
            "nte,nde->td", stacked_grads, attn_full[:3], preferred_element_type=jnp.float32
        )
    ).astype(jnp.bfloat16)
    grad_attention_full = jnp.concatenate([grad_qkv, grad_output_proj[None]], axis=0)
    vector_head = jnp.stack(
        [
            grad_gain_one,
            grad_gain_two,
            grad_shift_one,
            grad_shift_two,
            jnp.sum(grad_query.astype(jnp.float32), axis=0),
            jnp.sum(grad_values.astype(jnp.float32), axis=0),
            grad_bias_mixed,
            jnp.sum(grad_branch.astype(jnp.float32), axis=0),
        ]
    )
    grad_bias_up = jnp.sum(grad_pre_low.astype(jnp.float32), axis=0).reshape(FF // D, D)
    grad_vectors_full = jnp.concatenate([vector_head, grad_bias_up], axis=0)
    grad_attention, grad_vectors = (
        lax.psum_scatter(grad_attention_full, "fsdp", scatter_dimension=1, tiled=True),
        lax.psum_scatter(grad_vectors_full, "fsdp", scatter_dimension=1, tiled=True),
    )
    attention_new = inner_step(
        attention_weight, grad_attention, attention_first[0], attention_second[0], 0.03, 0.1
    )
    expand_new = inner_step(
        expand_weight, grad_expand, expand_first[0], expand_second[0], 0.03, 0.1
    )
    contract_new = inner_step(
        contract_weight, grad_contract, contract_first[0], contract_second[0], 0.015, 0.1
    )
    vectors_new = inner_step(vectors, grad_vectors, vectors_first[0], vectors_second[0], 0.2, 0.0)
    summed = (
        lax.psum((attention_weight - attention_new[0]).astype(jnp.bfloat16), "rep").astype(
            jnp.float32
        ),
        lax.psum((expand_weight - expand_new[0]).astype(jnp.bfloat16), "rep").astype(jnp.float32),
        lax.psum((contract_weight - contract_new[0]).astype(jnp.bfloat16), "rep").astype(
            jnp.float32
        ),
        lax.psum((vectors - vectors_new[0]).astype(jnp.bfloat16), "rep").astype(jnp.float32),
    )
    groups_count = lax.axis_size("rep")
    results = []
    for weight_now, momentum_now, inner_new, diff_total in zip(
        (attention_weight, expand_weight, contract_weight, vectors),
        (attention_momentum, expand_momentum, contract_momentum, vectors_momentum),
        (attention_new, expand_new, contract_new, vectors_new),
        summed,
    ):
        mean_diff = diff_total / groups_count
        momentum_new = 0.5 * momentum_now + mean_diff
        outer_new = weight_now - 0.7 * (mean_diff + 0.5 * momentum_new)
        results.append(
            (
                inner_new[1][None],
                inner_new[2][None],
                jnp.stack([mean_diff, momentum_new, outer_new]),
                outer_new.astype(jnp.bfloat16),
            )
        )
    return (
        layer_output.astype(jnp.bfloat16),
        input_grad,
        results[0][0],
        results[0][1],
        results[0][2],
        results[0][3],
        results[1][0],
        results[1][1],
        results[1][2],
        results[1][3],
        results[2][0],
        results[2][1],
        results[2][2],
        results[2][3],
        results[3][0],
        results[3][1],
        results[3][2],
        results[3][3],
    )


def solution(mesh):
    placed = (
        P(("rep", "fsdp"), None),
        P(("rep", "fsdp"), None),
        P(("rep", "fsdp"), None),
        P(None, "fsdp", None),
        P(None, "fsdp", None),
        P("rep", None, "fsdp", None),
        P("rep", None, "fsdp", None),
        P("fsdp", None),
        P("fsdp", None),
        P("rep", "fsdp", None),
        P("rep", "fsdp", None),
        P("fsdp", None),
        P("fsdp", None),
        P("rep", "fsdp", None),
        P("rep", "fsdp", None),
        P(None, "fsdp"),
        P(None, "fsdp"),
        P("rep", None, "fsdp"),
        P("rep", None, "fsdp"),
    )
    return jax.shard_map(
        per_device,
        mesh=mesh,
        in_specs=placed,
        out_specs=(
            P(("rep", "fsdp"), None),
            P(("rep", "fsdp"), None),
            P("rep", None, "fsdp", None),
            P("rep", None, "fsdp", None),
            P(None, None, "fsdp", None),
            P(None, "fsdp", None),
            P("rep", "fsdp", None),
            P("rep", "fsdp", None),
            P(None, "fsdp", None),
            P("fsdp", None),
            P("rep", "fsdp", None),
            P("rep", "fsdp", None),
            P(None, "fsdp", None),
            P("fsdp", None),
            P("rep", None, "fsdp"),
            P("rep", None, "fsdp"),
            P(None, None, "fsdp"),
            P(None, "fsdp"),
        ),
        check_vma=False,
    )
```

profile of v0, /device:TPU:0, one launch (start us, length us, event | category | flops | bytes accessed | tf_op | source)
XLA Modules:
  0.0 1465.5 jit_solution(9158751748262666368)
XLA Ops:
  16.3 28.9 %all_gather.13 = bf16[12,1024]{1,0:T(8,128)(2,1)S(1)} all-gather(bf16[12,128]{1,0:T(8,128)(2,1)S(1)} %convert_element_type.221), channel_id=1, replica_groups=mesh['rep'=4,'fsdp'=8] {'fsdp'}, dimensions={1}, use_global_device_ids=true | all-gather | bytes 27648 | tf_op jit(solution)/shard_map/all_gather | solution.py:88
  49.2 4.1 copy.37
  54.0 84.8 %all-gather.4.cloned.1.call-done = bf16[4,1024,1024]{1,2,0:T(8,128)(2,1)} async-done(((bf16[4,128,1024]{1,2,0:T(8,128)(2,1)}), bf16[4,1024,1024]{1,2,0:T(8,128)(2,1)}) %all-gather.4.cloned.1.call-update) | async-done | bytes 8388624 | tf_op jit(solution)/shard_map/all_gather | solution.py:87
  138.7 9.0 convolution_bitcast_fusion.1
  147.7 4.6 copy-done.29
  152.7 5.1 fusion.137
  158.2 8.4 select_reduce_fusion.1
  166.6 8.4 select_reduce_fusion.3
  176.6 13.4 fusion.6
  190.0 8.9 fusion.7
  201.7 6.9 fusion.77
  208.6 8.9 fusion.78
  217.6 13.5 fusion.8
  231.1 8.6 fusion.9
  242.1 4.9 fusion.75
  247.1 8.3 fusion.76
  255.6 4.3 fusion.140
  264.1 48.0 %multiply_convert_fusion.4 = (bf16[1024,4096]{1,0:T(8,128)(2,1)}, f32[1024,4096]{1,0:T(8,128)}, f32[1024,4096]{1,0:T(8,128)}) fusion(f32[4096]{0:T(1024)S(1)} %bitcast.308, bf16[1024,4096]{1,0:T(8,128)(2,1)} %all-gather.6.cloned.1.call-done, bf16[1024,1024]{0,1:T(8,128)(2,1)S(1)} %fusion.134.clone.4), kind=kOutput, calls=%fused_computation.17 | convolution fusion | flops 8866758656 | bytes 52445184 | tf_op jit(solution)/shard_map/dot_general | solution.py:150
  312.1 77.4 %all-gather.8.cloned.1.call-done = bf16[4096,1024]{1,0:T(8,128)(2,1)} async-done(((bf16[512,1024]{1,0:T(8,128)(2,1)}), bf16[4096,1024]{1,0:T(8,128)(2,1)}) %all-gather.8.cloned.1.call-update) | async-done | bytes 8388624 | tf_op jit(solution)/shard_map/all_gather | solution.py:148
  389.5 14.9 %fusion.141 = (f32[1024]{0:T(1024)S(1)}, f32[1024,1024]{0,1:T(8,128)S(1)}) fusion(f32[1024]{0:T(1024)S(1)} %bitcast.316, bf16[1024,4096]{1,0:T(8,128)(2,1)} %get-tuple-element.65, bf16[4096,1024]{1,0:T(8,128)(2,1)} %all-gather.8.cloned.1.call-done, f32[1024]{0:T(1024)S(1)} %bitcast.304, f32[1024]{0:T(1024)S(1)} %bitcast.294, ...), kind=kOutput, calls=%fused_computation.264 | convolution fusion | flops 8597273600 | bytes 25190400 | tf_op jit(solution)/shard_map/dot_general | solution.py:152
  410.4 4.3 convert_reduce_fusion.2
  414.7 24.3 %convert_reduce_fusion = (f32[4096]{0:T(1024)}, bf16[1024,4096]{1,0:T(8,128)(2,1)}) fusion(f32[1024,4096]{1,0:T(8,128)} %get-tuple-element.66, f32[1024,4096]{1,0:T(8,128)} %get-tuple-element.120, f32[4096]{0:T(1024)S(1)} %bitcast.309, bf16[1024,1024]{0,1:T(8,128)(2,1)} %get-tuple-element.60, bf16[4096,1024]{1,0:T(8,128)(2,1)} %all-gather.8.cloned.1.call-done), kind=kOutput, calls=%fused_computation.3 | convolution fusion | flops 8661233664 | bytes 52461568 | tf_op jit(solution)/shard_map/dot_general | solution.py:43
  439.0 14.9 %fusion.131 = f32[1024,4096]{1,0:T(8,128)} fusion(bf16[1024,4096]{1,0:T(8,128)(2,1)} %get-tuple-element.58, f32[1024,1024]{0,1:T(8,128)S(1)} %copy-done.7, f32[1024]{0:T(1024)S(1)} %bitcast.305, f32[1024]{0:T(1024)S(1)} %bitcast.295, f32[1024]{0:T(1024)S(1)} %add_rsqrt_fusion.1, f32[1024]{0:T(1024)S(1)} %broadcast_multiply_fusion.5), kind=kOutput, calls=%fused_computation.258 | convolution fusion | flops 8595177472 | bytes 29376512 | tf_op jit(solution)/shard_map/dot_general | solution.py:37
  455.5 19.6 %multiply_reduce_fusion.4 = (f32[1024]{0:T(1024)}, f32[1024]{0:T(1024)S(1)}, f32[1024]{0:T(1024)S(1)}, f32[1024]{0:T(1024)}, f32[1024,1024]{0,1:T(8,128)S(1)}) fusion(f32[1024,1024]{0,1:T(8,128)} %copy-done.6, f32[1024]{0:T(1024)S(1)} %add_rsqrt_fusion.1, f32[1024]{0:T(1024)S(1)} %broadcast_multiply_fusion.5, f32[1024]{0:T(1024)S(1)} %bitcast.296, ...), kind=kOutput, calls=%fused_computation.96 | convolution fusion | flops 8608804864 | bytes 31506432 | tf_op jit(solution)/shard_map/dot_general | solution.py:43
  477.4 5.6 convolution_convert_fusion
  483.0 9.9 fusion.14
  493.0 9.9 fusion.16
  502.9 6.7 fusion.84
  509.7 10.6 fusion.81
  522.0 4.1 copy.44
  526.0 9.4 fusion.95
  535.5 9.3 fusion.96
  544.8 21.2 %multiply_reduce_fusion.3 = (f32[8,512]{1,0:T(8,128)}, f32[8,512]{1,0:T(8,128)}, f32[8,512,1024]{2,1,0:T(8,128)}) fusion(f32[8,512,1024]{2,1,0:T(8,128)} %get-tuple-element.116, f32[8,512]{1,0:T(8,128)} %copy-done.50, pred[512,1024]{1,0:T(8,128)(4,1)S(1)} %copy-done.11, f32[8,512,1024]{2,1,0:T(8,128)} %fusion.96, f32[8,512]{1,0:T(8,128)} %copy-done.52, ...), kind=kOutput, calls=%fused_computation.14 | convolution fusion | flops 570417152 | bytes 69271552 | tf_op jit(solution)/shard_map/qhd,khd->hqk/dot_general | solution.py:207
  566.1 24.3 %multiply_reduce_fusion.1 = (f32[8,512]{1,0:T(8,128)S(1)}, f32[8,512]{1,0:T(8,128)S(1)}, f32[8,512,1024]{2,1,0:T(8,128)}) fusion(f32[8,512,1024]{2,1,0:T(8,128)} %get-tuple-element.113, f32[8,512]{1,0:T(8,128)} %copy-done.54, pred[512,1024]{1,0:T(8,128)(4,1)S(1)} %copy-done.13, f32[8,512,1024]{2,1,0:T(8,128)} %fusion.95, f32[8,512]{1,0:T(8,128)} %copy-done.56, ...), kind=kOutput, calls=%fused_computation.8 | convolution fusion | flops 570417152 | bytes 69271552 | tf_op jit(solution)/shard_map/qhd,khd->hqk/dot_general | solution.py:207
  590.5 52.7 %multiply_convert_fusion.1 = (bf16[8,512,1024]{2,1,0:T(8,128)(2,1)}, bf16[8,512,1024]{2,1,0:T(8,128)(2,1)S(1)}, bf16[8,512,1024]{2,1,0:T(8,128)(2,1)}, bf16[8,512,1024]{2,1,0:T(8,128)(2,1)}) fusion(f32[8,512,1024]{2,1,0:T(8,128)} %get-tuple-element.125, f32[8,512,1024]{2,1,0:T(8,128)} %get-tuple-element.113, f32[8,512]{1,0:T(8,128)S(1)} %get-tuple-element.44, ...), kind=kLoop, calls=%fused_computation.7 | loop fusion | flops 83886080 | bytes 168951808 | tf_op jit(solution)/shard_map/convert_element_type | solution.py:211
  643.2 8.2 fusion.103
  659.9 4.6 copy.43
  664.5 6.0 fusion.89
  670.5 6.2 fusion.90
  676.8 6.3 fusion.88
  695.4 6.9 convolution_bitcast_fusion
  702.3 6.1 pad_maximum_fusion
  710.0 14.9 %fusion.142 = f32[4096,1024]{1,0:T(8,128)} fusion(bf16[1024,4096]{1,0:T(8,128)(2,1)} %get-tuple-element.65, bf16[1024,1024]{0,1:T(8,128)(2,1)S(1)} %copy-done.45), kind=kOutput, calls=%fused_computation.265 | convolution fusion | flops 8589934592 | bytes 27262976 | tf_op jit(solution)/shard_map/dot_general | solution.py:37
  728.3 3.0 copy.47
  731.3 2.9 copy.50
  734.7 3.9 copy.57
  740.4 8.5 fusion.100
  748.9 266.6 %reduce-scatter.5.cloned.1.call-done = f32[4,128,1024]{1,2,0:T(8,128)} async-done(((f32[4,1024,1024]{1,2,0:T(8,128)}), f32[4,128,1024]{1,2,0:T(8,128)}) %reduce-scatter.5.cloned.1.call-update) | async-done | bytes 2097168 | tf_op jit(solution)/shard_map/reduce_scatter | solution.py:254
  1015.5 6.2 fusion.50
  1021.7 276.8 %reduce-scatter.9.cloned.1.call-done = f32[512,1024]{1,0:T(8,128)} async-done(((f32[4096,1024]{1,0:T(8,128)}), f32[512,1024]{1,0:T(8,128)}) %reduce-scatter.9.cloned.1.call-update) | async-done | bytes 2097168 | tf_op jit(solution)/shard_map/reduce_scatter | solution.py:166
  1298.5 7.8 fusion.99
  1306.4 13.0 fusion.47
  1319.4 4.0 copy.58
  1323.4 32.2 %reduce-scatter.11.cloned.1.call-done = f32[12,128]{1,0:T(8,128)} async-done(((f32[12,1024]{1,0:T(8,128)}), f32[12,128]{1,0:T(8,128)}) %reduce-scatter.11.cloned.1.call-update) | async-done | bytes 6160 | tf_op jit(solution)/shard_map/reduce_scatter | solution.py:255
  1357.5 5.9 psum.31
  1364.7 2.9 copy.60
  1367.5 2.9 copy.59
  1370.4 56.4 %all-reduce.3.cloned.1.call-done = (bf16[4,128,1024]{1,2,0:T(8,128)(2,1)}, bf16[128,4096]{1,0:T(8,128)(2,1)}, bf16[512,1024]{1,0:T(8,128)(2,1)}) async-done(((bf16[4,128,1024]{1,2,0:T(8,128)(2,1)}, bf16[128,4096]{1,0:T(8,128)(2,1)}, bf16[512,1024]{1,0:T(8,128)(2,1)}), (bf16[4,128,1024]{1,2,0:T(8,128)(2,1)}, bf16[128,4096]{1,0:T(8,128)(2,1)}, bf16[512,1024]{1,0:T(8,128)(2,1)})) %all-reduce.3.cloned.1.call-update) | async-done | bytes 3145744 | tf_op jit(solution)/shard_map/psum | solution.py:268
  1426.8 5.0 fusion.125
  1433.1 6.0 pad_maximum_fusion.2
  1439.1 6.7 copy.61
  1445.8 3.6 fusion.127
  1451.7 3.1 pad_maximum_fusion.3
  1454.8 3.3 pad_maximum_fusion.4
  (297 shorter events, 71.4 us)
Async XLA Ops:
  7.2 131.6 %all-gather.4.cloned.1.call-start = ((), (), s32[]{:S(2)}) async-start(), calls=%async_computation.4 | async-start | bytes 9437184 | tf_op jit(solution)/shard_map/all_gather | solution.py:87
  10.5 35.4 %copy-start.84 = (s32[1,1024]{1,0:T(1,128)S(1)}, s32[1,1024]{1,0:T(1,128)}, u32[]{:S(2)}) copy-start(s32[1,1024]{1,0:T(1,128)} %param.21) | copy-start | bytes 12292
  10.5 253.7 %all-gather.6.cloned.1.call-start = ((), (), s32[]{:S(2)}) async-start(), calls=%async_computation.5 | async-start | bytes 9437184 | tf_op jit(solution)/shard_map/all_gather | solution.py:147
  13.3 376.3 %all-gather.8.cloned.1.call-start = ((), (), s32[]{:S(2)}) async-start(), calls=%async_computation.6 | async-start | bytes 9437184 | tf_op jit(solution)/shard_map/all_gather | solution.py:148
  13.3 33.4 %copy-start.36 = (bf16[1024,1024]{1,0:T(8,128)(2,1)S(1)}, bf16[1024,1024]{1,0:T(8,128)(2,1)}, u32[]{:S(2)}) copy-start(bf16[1024,1024]{1,0:T(8,128)(2,1)} %param.20) | copy-start | bytes 6291460
  16.2 724.2 %reduce-scatter.7.cloned.1.call-start = ((), (), s32[]{:S(2)}) async-start(), calls=%async_computation.8 | async-start | bytes 18874368 | tf_op jit(solution)/shard_map/reduce_scatter | solution.py:165
  49.2 89.5 %copy-start.37 = (bf16[1024,1024]{1,0:T(8,128)(2,1)S(1)}, bf16[1024,1024]{1,0:T(8,128)(2,1)}, u32[]{:S(2)}) copy-start(bf16[1024,1024]{1,0:T(8,128)(2,1)} %param.19) | copy-start | bytes 6291460
  54.0 154.6 %copy-start.10 = (pred[512,1024]{1,0:T(8,128)(4,1)}, pred[512,1024]{1,0:T(8,128)(4,1)S(1)}, u32[]{:S(2)}) copy-start(pred[512,1024]{1,0:T(8,128)(4,1)S(1)} %get-tuple-element.108) | copy-start | bytes 1572868
  54.0 193.1 %copy-start.12 = (pred[512,1024]{1,0:T(8,128)(4,1)}, pred[512,1024]{1,0:T(8,128)(4,1)S(1)}, u32[]{:S(2)}) copy-start(pred[512,1024]{1,0:T(8,128)(4,1)S(1)} %get-tuple-element.109) | copy-start | bytes 1572868
  152.7 64.9 %copy-start.4 = (bf16[1,1024,1024]{1,2,0:T(8,128)(2,1)}, bf16[1,1024,1024]{1,2,0:T(8,128)(2,1)S(1)}, u32[]{:S(2)}) copy-start(bf16[1,1024,1024]{1,2,0:T(8,128)(2,1)S(1)} %slice.220) | copy-start | bytes 6291460
  158.2 59.4 %copy-start.16 = (bf16[1,1024,16,64]{1,3,2,0:T(8,128)(2,1)}, bf16[1,1024,16,64]{1,3,2,0:T(8,128)(2,1)S(1)}, u32[]{:S(2)}) copy-start(bf16[1,1024,16,64]{1,3,2,0:T(8,128)(2,1)S(1)} %multiply_convert_fusion.5) | copy-start | bytes 6291460
  166.6 80.5 %copy-start.58 = (f32[8,512]{1,0:T(8,128)}, f32[8,512]{1,0:T(8,128)S(1)}, u32[]{:S(2)}) copy-start(f32[8,512]{1,0:T(8,128)S(1)} %get-tuple-element.112) | copy-start | bytes 49156
  175.0 33.6 %copy-start.60 = (f32[8,512]{1,0:T(8,128)}, f32[8,512]{1,0:T(8,128)S(1)}, u32[]{:S(2)}) copy-start(f32[8,512]{1,0:T(8,128)S(1)} %get-tuple-element.115) | copy-start | bytes 49156
  190.0 8.9 copy-start.62
  190.0 18.6 %copy-start.70 = (f32[8,512]{1,0:T(8,128)}, f32[8,512]{1,0:T(8,128)S(1)}, u32[]{:S(2)}) copy-start(f32[8,512]{1,0:T(8,128)S(1)} %get-tuple-element.48) | copy-start | bytes 49156
  190.0 11.7 copy-start
  217.6 22.1 %copy-start.18 = (bf16[1,1024,16,64]{1,3,2,0:T(8,128)(2,1)S(1)}, bf16[1,1024,16,64]{1,3,2,0:T(8,128)(2,1)}, u32[]{:S(2)}) copy-start(bf16[1,1024,16,64]{1,3,2,0:T(8,128)(2,1)} %add_convert_fusion.2) | copy-start | bytes 6291460
  231.1 16.0 %copy-start.72 = (f32[8,512]{1,0:T(8,128)}, f32[8,512]{1,0:T(8,128)S(1)}, u32[]{:S(2)}) copy-start(f32[8,512]{1,0:T(8,128)S(1)} %get-tuple-element.50) | copy-start | bytes 49156
  231.1 11.0 copy-start.1
  264.1 125.4 %copy-start.94 = (f32[1,1024]{1,0:T(1,128)S(1)}, f32[1,1024]{1,0:T(1,128)}, u32[]{:S(2)}) copy-start(f32[1,1024]{1,0:T(1,128)} %get-tuple-element.99) | copy-start | bytes 12292
  414.7 24.3 %copy-start.7 = (f32[1024,1024]{0,1:T(8,128)S(1)}, f32[1024,1024]{0,1:T(8,128)}, u32[]{:S(2)}) copy-start(f32[1024,1024]{0,1:T(8,128)} %copy-done.6) | copy-start | bytes 12582916
  454.0 21.2 %copy-start.61 = (f32[8,512]{1,0:T(8,128)S(1)}, f32[8,512]{1,0:T(8,128)}, u32[]{:S(2)}) copy-start(f32[8,512]{1,0:T(8,128)} %copy-done.60) | copy-start | bytes 49156
  454.0 21.2 %copy-start.71 = (f32[8,512]{1,0:T(8,128)S(1)}, f32[8,512]{1,0:T(8,128)}, u32[]{:S(2)}) copy-start(f32[8,512]{1,0:T(8,128)} %copy-done.70) | copy-start | bytes 49156
  454.0 21.2 %copy-start.63 = (f32[8,512]{1,0:T(8,128)S(1)}, f32[8,512]{1,0:T(8,128)}, u32[]{:S(2)}) copy-start(f32[8,512]{1,0:T(8,128)} %copy-done.62) | copy-start | bytes 49156
  454.0 21.2 %copy-start.75 = (f32[8,512]{1,0:T(8,128)S(1)}, f32[8,512]{1,0:T(8,128)}, u32[]{:S(2)}) copy-start(f32[8,512]{1,0:T(8,128)} %copy-done.74) | copy-start | bytes 49156
  454.0 21.2 %copy-start.59 = (f32[8,512]{1,0:T(8,128)S(1)}, f32[8,512]{1,0:T(8,128)}, u32[]{:S(2)}) copy-start(f32[8,512]{1,0:T(8,128)} %copy-done.58) | copy-start | bytes 49156
  454.0 21.2 %copy-start.73 = (f32[8,512]{1,0:T(8,128)S(1)}, f32[8,512]{1,0:T(8,128)}, u32[]{:S(2)}) copy-start(f32[8,512]{1,0:T(8,128)} %copy-done.72) | copy-start | bytes 49156
  454.0 21.3 %copy-start.65 = (f32[8,512]{1,0:T(8,128)S(1)}, f32[8,512]{1,0:T(8,128)}, u32[]{:S(2)}) copy-start(f32[8,512]{1,0:T(8,128)} %copy-done.64) | copy-start | bytes 49156
  454.0 21.3 %copy-start.77 = (f32[8,512]{1,0:T(8,128)S(1)}, f32[8,512]{1,0:T(8,128)}, u32[]{:S(2)}) copy-start(f32[8,512]{1,0:T(8,128)} %copy-done.76) | copy-start | bytes 49156
  454.0 561.5 %reduce-scatter.5.cloned.1.call-start = ((), (), s32[]{:S(2)}) async-start(), calls=%async_computation.7 | async-start | bytes 18874368 | tf_op jit(solution)/shard_map/reduce_scatter | solution.py:254
  455.5 19.8 %copy-start.8 = (f32[1024,1024]{0,1:T(8,128)S(1)}, f32[1024,1024]{0,1:T(8,128)}, u32[]{:S(2)}) copy-start(f32[1024,1024]{0,1:T(8,128)} %copy-done.6) | copy-start | bytes 12582916
  475.2 34.4 %copy-start.50 = (f32[8,512]{1,0:T(8,128)}, f32[8,512]{1,0:T(8,128)S(1)}, u32[]{:S(2)}) copy-start(f32[8,512]{1,0:T(8,128)S(1)} %log_add_fusion.3) | copy-start | bytes 49156
  475.3 27.6 %copy-start.52 = (f32[8,512]{1,0:T(8,128)}, f32[8,512]{1,0:T(8,128)S(1)}, u32[]{:S(2)}) copy-start(f32[8,512]{1,0:T(8,128)S(1)} %log_add_fusion.2) | copy-start | bytes 49156
  475.3 17.7 %copy-start.54 = (f32[8,512]{1,0:T(8,128)}, f32[8,512]{1,0:T(8,128)S(1)}, u32[]{:S(2)}) copy-start(f32[8,512]{1,0:T(8,128)S(1)} %log_add_fusion.1) | copy-start | bytes 49156
  483.0 10.0 copy-start.30
  483.0 19.9 %slice-start = ((s8[16777216]{0:T(1024)(128)(4,1)}), s8[4194304]{0:T(1024)(128)(4,1)S(1)}, s32[]{:S(2)}) async-start(s8[16777216]{0:T(1024)(128)(4,1)} %bitcast.261), calls=%async_computation.12 | async-start | bytes 8388608
  483.0 19.9 %slice-start.1 = ((s8[16777216]{0:T(1024)(128)(4,1)}), s8[4194304]{0:T(1024)(128)(4,1)S(1)}, s32[]{:S(2)}) async-start(s8[16777216]{0:T(1024)(128)(4,1)} %bitcast.261), calls=%async_computation.13 | async-start | bytes 8388608
  493.0 9.9 slice-start.2
  493.0 9.9 slice-start.3
  493.0 9.9 copy-start.11
  509.7 10.6 copy-start.25
  526.0 9.5 copy-start.20
  526.0 18.8 %slice-start.4 = ((s8[16777216]{0:T(1024)(128)(4,1)}), s8[4194304]{0:T(1024)(128)(4,1)S(1)}, s32[]{:S(2)}) async-start(s8[16777216]{0:T(1024)(128)(4,1)} %bitcast.263), calls=%async_computation.16 | async-start | bytes 8388608
  526.0 18.8 %slice-start.5 = ((s8[16777216]{0:T(1024)(128)(4,1)}), s8[4194304]{0:T(1024)(128)(4,1)S(1)}, s32[]{:S(2)}) async-start(s8[16777216]{0:T(1024)(128)(4,1)} %bitcast.263), calls=%async_computation.17 | async-start | bytes 8388608
  535.5 9.4 slice-start.6
  535.5 9.4 slice-start.7
  566.1 24.4 %copy-start.51 = (f32[8,512]{1,0:T(8,128)S(1)}, f32[8,512]{1,0:T(8,128)}, u32[]{:S(2)}) copy-start(f32[8,512]{1,0:T(8,128)} %copy-done.50) | copy-start | bytes 49156
  566.1 24.4 %copy-start.53 = (f32[8,512]{1,0:T(8,128)S(1)}, f32[8,512]{1,0:T(8,128)}, u32[]{:S(2)}) copy-start(f32[8,512]{1,0:T(8,128)} %copy-done.52) | copy-start | bytes 49156
  566.1 24.4 %copy-start.55 = (f32[8,512]{1,0:T(8,128)S(1)}, f32[8,512]{1,0:T(8,128)}, u32[]{:S(2)}) copy-start(f32[8,512]{1,0:T(8,128)} %copy-done.54) | copy-start | bytes 49156
  566.1 24.4 %copy-start.57 = (f32[8,512]{1,0:T(8,128)S(1)}, f32[8,512]{1,0:T(8,128)}, u32[]{:S(2)}) copy-start(f32[8,512]{1,0:T(8,128)} %copy-done.56) | copy-start | bytes 49156
  566.1 24.4 %copy-start.68 = (f32[8,512]{1,0:T(8,128)S(1)}, f32[8,512]{1,0:T(8,128)}, u32[]{:S(2)}) copy-start(f32[8,512]{1,0:T(8,128)} %get-tuple-element.46) | copy-start | bytes 49156
  566.1 24.4 %copy-start.69 = (f32[8,512]{1,0:T(8,128)S(1)}, f32[8,512]{1,0:T(8,128)}, u32[]{:S(2)}) copy-start(f32[8,512]{1,0:T(8,128)} %get-tuple-element.47) | copy-start | bytes 49156
  643.2 11.3 copy-start.2
  643.2 9.1 copy-start.3
  643.2 9.7 copy-start.17
  670.5 12.5 slice-start.10
  708.5 590.0 %reduce-scatter.9.cloned.1.call-start = ((), (), s32[]{:S(2)}) async-start(), calls=%async_computation.9 | async-start | bytes 18874368 | tf_op jit(solution)/shard_map/reduce_scatter | solution.py:166
  724.9 630.6 %reduce-scatter.11.cloned.1.call-start = ((), (), s32[]{:S(2)}) async-start(), calls=%async_computation.10 | async-start | bytes 73728 | tf_op jit(solution)/shard_map/reduce_scatter | solution.py:255
  740.1 275.4 %copy-start.15 = (f32[4,128,1024]{1,2,0:T(8,128)S(1)}, f32[4,128,1024]{1,2,0:T(8,128)}, u32[]{:S(2)}) copy-start(f32[4,128,1024]{1,2,0:T(8,128)} %copy-done.14) | copy-start | bytes 6291460
  740.1 686.7 %all-reduce.3.cloned.1.call-start = ((), (), s32[]{:S(2)}) async-start(), calls=%async_computation.11 | async-start | bytes 6291456 | tf_op jit(solution)/shard_map/psum | solution.py:268
  1319.4 36.2 %copy-start.67 = (f32[12,128]{1,0:T(8,128)S(1)}, f32[12,128]{1,0:T(8,128)}, u32[]{:S(2)}) copy-start(f32[12,128]{1,0:T(8,128)} %param.34) | copy-start | bytes 18436
  1319.4 36.2 %copy-start.90 = (f32[1,12,128]{2,0,1:T(1,128)S(1)}, f32[1,12,128]{2,0,1:T(1,128)}, u32[]{:S(2)}) copy-start(f32[1,12,128]{2,0,1:T(1,128)} %param.36) | copy-start | bytes 18436
  1319.4 36.2 %copy-start.91 = (f32[1,12,128]{2,0,1:T(1,128)S(1)}, f32[1,12,128]{2,0,1:T(1,128)}, u32[]{:S(2)}) copy-start(f32[1,12,128]{2,0,1:T(1,128)} %param.37) | copy-start | bytes 18436
  1319.4 44.0 %copy-start.89 = (f32[12,128]{1,0:T(8,128)S(1)}, f32[12,128]{1,0:T(8,128)}, u32[]{:S(2)}) copy-start(f32[12,128]{1,0:T(8,128)} %param.35) | copy-start | bytes 18436
  (52 other events, 237.5 us)
Sparse Core Ops, SparseCore 0:
  10.6 128.0 all-gather.3
  141.4 122.6 all-gather.5
  266.8 122.6 all-gather.7
  454.1 278.3 reduce-scatter.6
  736.1 279.3 reduce-scatter.4
  1019.1 279.3 reduce-scatter.8
  1301.6 53.9 reduce-scatter.10
  1359.3 67.5 all-reduce.2
where the time goes:
time: 1480 us; the launch traced here: 1470 us
  waiting for transfers between devices  796 us (54%)
  matrix products  386 us (26%)
  other arithmetic  150 us (10%)
  local copies, waits for them, and re-layouts  82.1 us (6%)
  blocking collectives  34.9 us (2%)
  between operations  16 us (1%)
    reduce_scatter x1, waiting for transfers between devices, per_device(): lax.psum_scatter(contract_full, 'fsdp', scatter_dimension=0, tiled=True)  277 us
    reduce_scatter x1, waiting for transfers between devices, per_device(): lax.psum_scatter(grad_attention_full, 'fsdp', scatter_dimension=1, tiled=...  267 us
    all_gather x1, waiting for transfers between devices, per_device(): lax.all_gather(attention_weight.astype(jnp.bfloat16), 'fsdp', axis=1, til...  84.8 us
    all_gather x1, waiting for transfers between devices, per_device(): lax.all_gather(contract_weight.astype(jnp.bfloat16), 'fsdp', axis=0, tile...  77.4 us
    dot_general x4, matrix products, per_device(): jnp.einsum('qhd,khd->hqk', ctx_grad, value_block, preferred_element_type=...  64.3 us
    unnamed x230, local copies, waits for them, and re-layouts  62 us
    psum x1, waiting for transfers between devices, per_device(): lax.psum((attention_weight - attention_new[0]).astype(jnp.bfloat16), 'rep')  56.4 us
    convert_element_type x1, other arithmetic, per_device(): score_grad = (probability * (prob_grad - row_dot)).astype(jnp.bfloat16)  52.7 us
  transfers between devices with their start and end apart: 8, of which 7 were waited for; matrix products, arithmetic and copies ran while one was open for 34% of the time, Pallas kernels for 0%

commit v1 on v0

--- a/solution.py
+++ b/solution.py
@@ -265,9 +265,10 @@
     )
     vectors_new = inner_step(vectors, grad_vectors, vectors_first[0], vectors_second[0], 0.2, 0.0)
     summed = (
-        lax.psum((attention_weight - attention_new[0]).astype(jnp.bfloat16), "rep").astype(
-            jnp.float32
-        ),
+        jnp.sum(
+            lax.all_gather((attention_weight - attention_new[0]).astype(jnp.bfloat16), "rep"),
+            axis=0,
+        ).astype(jnp.float32),
         lax.psum((expand_weight - expand_new[0]).astype(jnp.bfloat16), "rep").astype(jnp.float32),
         lax.psum((contract_weight - contract_new[0]).astype(jnp.bfloat16), "rep").astype(
             jnp.float32

time: 1480 us -> 1480 us (level)
    all_gather x0 -> x1, waiting for transfers between devices: none -> 22.4 us  [per_device(): lax.all_gather((attention_weight - attention_new[0]).astype(jnp.bfloat16)...]
    psum x1, waiting for transfers between devices: 56.4 us -> 38.6 us  [per_device(): lax.psum((expand_weight - expand_new[0]).astype(jnp.bfloat16), 'rep')]
    unnamed x230 -> x212, local copies, waits for them, and re-layouts: 62 us -> 59.1 us
  transfers between devices with their start and end apart: 8 -> 9, of which waited for: 7 -> 8; matrix products, arithmetic and copies ran while one was open for 34% -> 35% of each run, Pallas kernels for 0% -> 0%
where the time goes in v1:
time: 1480 us; the launch traced here: 1470 us
  waiting for transfers between devices  796 us (54%)
  matrix products  386 us (26%)
  other arithmetic  154 us (10%)
  local copies, waits for them, and re-layouts  83.5 us (6%)
  blocking collectives  34.9 us (2%)
  between operations  15.6 us (1%)
    reduce_scatter x1, waiting for transfers between devices, per_device(): lax.psum_scatter(contract_full, 'fsdp', scatter_dimension=0, tiled=True)  276 us
    reduce_scatter x1, waiting for transfers between devices, per_device(): lax.psum_scatter(grad_attention_full, 'fsdp', scatter_dimension=1, tiled=...  270 us
    all_gather x1, waiting for transfers between devices, per_device(): lax.all_gather(attention_weight.astype(jnp.bfloat16), 'fsdp', axis=1, til...  84.9 us
    all_gather x1, waiting for transfers between devices, per_device(): lax.all_gather(contract_weight.astype(jnp.bfloat16), 'fsdp', axis=0, tile...  77.1 us
    dot_general x4, matrix products, per_device(): jnp.einsum('qhd,khd->hqk', ctx_grad, value_block, preferred_element_type=...  63.8 us
    unnamed x212, local copies, waits for them, and re-layouts  59.1 us
    convert_element_type x1, other arithmetic, per_device(): score_grad = (probability * (prob_grad - row_dot)).astype(jnp.bfloat16)  52.5 us
    dot_general x3, matrix products, product_back(): lax.dot_general(left, right, (((1,), (1,)), ((), ())), preferred_element_...  49.1 us
  transfers between devices with their start and end apart: 9, of which 8 were waited for; matrix products, arithmetic and copies ran while one was open for 35% of the time, Pallas kernels for 0%

profile of v1, /device:TPU:0, one launch (start us, length us, event | category | flops | bytes accessed | tf_op | source)
XLA Modules:
  0.0 1471.2 jit_solution(12136680983258783926)
XLA Ops:
  16.3 28.9 %all_gather.19 = bf16[12,1024]{1,0:T(8,128)(2,1)S(1)} all-gather(bf16[12,128]{1,0:T(8,128)(2,1)S(1)} %convert_element_type.231), channel_id=1, replica_groups=mesh['rep'=4,'fsdp'=8] {'fsdp'}, dimensions={1}, use_global_device_ids=true | all-gather | bytes 27648 | tf_op jit(solution)/shard_map/all_gather | solution.py:88
  46.0 3.9 copy.90
  53.8 84.9 %all-gather.6.cloned.1.call-done = bf16[4,1024,1024]{1,2,0:T(8,128)(2,1)} async-done(((bf16[4,128,1024]{1,2,0:T(8,128)(2,1)}), bf16[4,1024,1024]{1,2,0:T(8,128)(2,1)}) %all-gather.6.cloned.1.call-update) | async-done | bytes 8388624 | tf_op jit(solution)/shard_map/all_gather | solution.py:87
  138.7 9.7 convolution_bitcast_fusion.1
  148.4 4.6 copy-done.24
  153.0 3.3 fusion.137
  159.2 8.4 select_reduce_fusion.3
  167.6 13.5 fusion.6
  181.1 8.0 fusion.7
  189.2 5.4 add_convert_fusion.2
  194.6 6.9 fusion.77
  201.5 9.0 fusion.78
  210.5 8.4 select_reduce_fusion.1
  219.0 13.8 fusion.8
  232.8 8.1 fusion.9
  243.8 4.9 fusion.75
  248.9 8.5 fusion.76
  257.5 4.3 fusion.140
  264.6 47.8 %multiply_convert_fusion.4 = (bf16[1024,4096]{1,0:T(8,128)(2,1)}, f32[1024,4096]{1,0:T(8,128)}, f32[1024,4096]{1,0:T(8,128)}) fusion(f32[4096]{0:T(1024)S(1)} %bitcast.312, bf16[1024,4096]{1,0:T(8,128)(2,1)} %all-gather.8.cloned.1.call-done, bf16[1024,1024]{0,1:T(8,128)(2,1)S(1)} %fusion.134.clone.4), kind=kOutput, calls=%fused_computation.17 | convolution fusion | flops 8866758656 | bytes 52445184 | tf_op jit(solution)/shard_map/dot_general | solution.py:150
  312.4 77.1 %all-gather.10.cloned.1.call-done = bf16[4096,1024]{1,0:T(8,128)(2,1)} async-done(((bf16[512,1024]{1,0:T(8,128)(2,1)}), bf16[4096,1024]{1,0:T(8,128)(2,1)}) %all-gather.10.cloned.1.call-update) | async-done | bytes 8388624 | tf_op jit(solution)/shard_map/all_gather | solution.py:148
  389.5 15.1 %fusion.141 = (f32[1024]{0:T(1024)S(1)}, f32[1024,1024]{0,1:T(8,128)S(1)}) fusion(f32[1024]{0:T(1024)S(1)} %bitcast.320, bf16[1024,4096]{1,0:T(8,128)(2,1)} %get-tuple-element.100, bf16[4096,1024]{1,0:T(8,128)(2,1)} %all-gather.10.cloned.1.call-done, f32[1024]{0:T(1024)S(1)} %bitcast.307, f32[1024]{0:T(1024)S(1)} %bitcast.298, ...), kind=kOutput, calls=%fused_computation.264 | convolution fusion | flops 8597273600 | bytes 25190400 | tf_op jit(solution)/shard_map/dot_general | solution.py:152
  410.6 4.1 convert_reduce_fusion.2
  414.6 24.6 %convert_reduce_fusion = (f32[4096]{0:T(1024)}, bf16[1024,4096]{1,0:T(8,128)(2,1)}) fusion(f32[1024,4096]{1,0:T(8,128)} %get-tuple-element.101, f32[1024,4096]{1,0:T(8,128)} %get-tuple-element.155, f32[4096]{0:T(1024)S(1)} %bitcast.313, bf16[1024,1024]{0,1:T(8,128)(2,1)} %get-tuple-element.95, bf16[4096,1024]{1,0:T(8,128)(2,1)} %all-gather.10.cloned.1.call-done), kind=kOutput, calls=%fused_computation.3 | convolution fusion | flops 8661233664 | bytes 52461568 | tf_op jit(solution)/shard_map/dot_general | solution.py:43
  439.3 15.0 %fusion.131 = f32[1024,4096]{1,0:T(8,128)} fusion(bf16[1024,4096]{1,0:T(8,128)(2,1)} %get-tuple-element.93, f32[1024,1024]{0,1:T(8,128)S(1)} %copy-done.6, f32[1024]{0:T(1024)S(1)} %bitcast.308, f32[1024]{0:T(1024)S(1)} %bitcast.299, f32[1024]{0:T(1024)S(1)} %add_rsqrt_fusion.1, f32[1024]{0:T(1024)S(1)} %broadcast_multiply_fusion.5), kind=kOutput, calls=%fused_computation.258 | convolution fusion | flops 8595177472 | bytes 29376512 | tf_op jit(solution)/shard_map/dot_general | solution.py:37
  455.8 15.2 %fusion.142 = f32[4096,1024]{1,0:T(8,128)} fusion(bf16[1024,4096]{1,0:T(8,128)(2,1)} %get-tuple-element.100, bf16[1024,1024]{0,1:T(8,128)(2,1)S(1)} %copy-done.39), kind=kOutput, calls=%fused_computation.265 | convolution fusion | flops 8589934592 | bytes 27262976 | tf_op jit(solution)/shard_map/dot_general | solution.py:37
  472.6 18.8 %multiply_reduce_fusion.4 = (f32[1024]{0:T(1024)}, f32[1024]{0:T(1024)S(1)}, f32[1024]{0:T(1024)S(1)}, f32[1024]{0:T(1024)}, f32[1024,1024]{0,1:T(8,128)S(1)}) fusion(f32[1024,1024]{0,1:T(8,128)} %copy-done.5, f32[1024]{0:T(1024)S(1)} %add_rsqrt_fusion.1, f32[1024]{0:T(1024)S(1)} %broadcast_multiply_fusion.5, f32[1024]{0:T(1024)S(1)} %bitcast.300, ...), kind=kOutput, calls=%fused_computation.96 | convolution fusion | flops 8608804864 | bytes 31506432 | tf_op jit(solution)/shard_map/dot_general | solution.py:43
  495.9 5.7 convolution_convert_fusion
  501.7 9.0 fusion.96
  510.7 8.5 fusion.95
  519.2 21.0 %multiply_reduce_fusion.3 = (f32[8,512]{1,0:T(8,128)}, f32[8,512]{1,0:T(8,128)}, f32[8,512,1024]{2,1,0:T(8,128)}) fusion(f32[8,512,1024]{2,1,0:T(8,128)} %get-tuple-element.151, f32[8,512]{1,0:T(8,128)} %log_add_fusion.3, pred[512,1024]{1,0:T(8,128)(4,1)S(1)} %copy-done.10, f32[8,512,1024]{2,1,0:T(8,128)} %fusion.96, f32[8,512]{1,0:T(8,128)} %log_add_fusion.2, ...), kind=kOutput, calls=%fused_computation.14 | convolution fusion | flops 570417152 | bytes 69271552 | tf_op jit(solution)/shard_map/qhd,khd->hqk/dot_general | solution.py:207
  540.2 25.4 %multiply_reduce_fusion.1 = (f32[8,512]{1,0:T(8,128)S(1)}, f32[8,512]{1,0:T(8,128)S(1)}, f32[8,512,1024]{2,1,0:T(8,128)}) fusion(f32[8,512,1024]{2,1,0:T(8,128)} %get-tuple-element.148, f32[8,512]{1,0:T(8,128)} %log_add_fusion.1, pred[512,1024]{1,0:T(8,128)(4,1)S(1)} %copy-done.12, f32[8,512,1024]{2,1,0:T(8,128)} %fusion.95, f32[8,512]{1,0:T(8,128)} %log_add_fusion, ...), kind=kOutput, calls=%fused_computation.8 | convolution fusion | flops 570417152 | bytes 69271552 | tf_op jit(solution)/shard_map/qhd,khd->hqk/dot_general | solution.py:207
  565.6 52.5 %multiply_convert_fusion.1 = (bf16[8,512,1024]{2,1,0:T(8,128)(2,1)}, bf16[8,512,1024]{2,1,0:T(8,128)(2,1)S(1)}, bf16[8,512,1024]{2,1,0:T(8,128)(2,1)}, bf16[8,512,1024]{2,1,0:T(8,128)(2,1)}) fusion(f32[8,512,1024]{2,1,0:T(8,128)} %get-tuple-element.160, f32[8,512,1024]{2,1,0:T(8,128)} %get-tuple-element.148, f32[8,512]{1,0:T(8,128)S(1)} %get-tuple-element.80, ...), kind=kLoop, calls=%fused_computation.7 | loop fusion | flops 83886080 | bytes 168951808 | tf_op jit(solution)/shard_map/convert_element_type | solution.py:211
  618.2 9.7 fusion.87
  627.9 6.2 fusion.88
  641.2 4.3 copy.95
  645.6 5.1 fusion.102
  650.7 5.1 fusion.103
  661.3 4.1 copy.96
  665.4 9.1 fusion.16
  674.6 9.5 fusion.14
  684.1 10.6 fusion.81
  694.8 6.7 fusion.84
  704.3 4.1 copy.97
  714.5 6.9 convolution_bitcast_fusion
  721.4 6.1 pad_maximum_fusion
  732.8 7.0 fusion.52
  739.8 276.0 %reduce-scatter.9.cloned.1.call-done = f32[512,1024]{1,0:T(8,128)} async-done(((f32[4096,1024]{1,0:T(8,128)}), f32[512,1024]{1,0:T(8,128)}) %reduce-scatter.9.cloned.1.call-update) | async-done | bytes 2097168 | tf_op jit(solution)/shard_map/reduce_scatter | solution.py:166
  1015.8 7.2 fusion.99
  1023.2 3.1 copy.100
  1029.2 269.6 %reduce-scatter.5.cloned.1.call-done = f32[4,128,1024]{1,2,0:T(8,128)} async-done(((f32[4,1024,1024]{1,2,0:T(8,128)}), f32[4,128,1024]{1,2,0:T(8,128)}) %reduce-scatter.5.cloned.1.call-update) | async-done | bytes 2097168 | tf_op jit(solution)/shard_map/reduce_scatter | solution.py:254
  1298.7 6.5 fusion.50
  1309.5 12.9 fusion.47
  1322.4 4.0 copy.113
  1326.4 3.9 copy.112
  1330.3 25.5 %reduce-scatter.11.cloned.1.call-done = f32[12,128]{1,0:T(8,128)} async-done(((f32[12,1024]{1,0:T(8,128)}), f32[12,128]{1,0:T(8,128)}) %reduce-scatter.11.cloned.1.call-update) | async-done | bytes 6160 | tf_op jit(solution)/shard_map/reduce_scatter | solution.py:255
  1357.8 5.9 psum.23
  1370.7 38.6 %all-reduce.3.cloned.1.call-done = (bf16[128,4096]{1,0:T(8,128)(2,1)}, bf16[512,1024]{1,0:T(8,128)(2,1)}) async-done(((bf16[128,4096]{1,0:T(8,128)(2,1)}, bf16[512,1024]{1,0:T(8,128)(2,1)}), (bf16[128,4096]{1,0:T(8,128)(2,1)}, bf16[512,1024]{1,0:T(8,128)(2,1)})) %all-reduce.3.cloned.1.call-update) | async-done | bytes 2097168 | tf_op jit(solution)/shard_map/psum | solution.py:272
  1409.3 4.4 fusion.129
  1413.7 3.8 pad_maximum_fusion.4
  1420.5 3.1 pad_maximum_fusion.3
  1423.6 22.4 %all-gather.12.cloned.1.call-done = bf16[16,128,1024]{2,1,0:T(8,128)(2,1)} async-done(((bf16[4,128,1024]{2,1,0:T(8,128)(2,1)}), bf16[16,128,1024]{2,1,0:T(8,128)(2,1)}) %all-gather.12.cloned.1.call-update) | async-done | bytes 4194320 | tf_op jit(solution)/shard_map/all_gather | solution.py:269
  1446.0 3.3 reduce_sum.253
  1453.2 3.1 pad_maximum_fusion.2
  1456.3 6.6 copy.116
  (286 shorter events, 86.8 us)
Async XLA Ops:
  7.2 131.5 %all-gather.6.cloned.1.call-start = ((), (), s32[]{:S(2)}) async-start(), calls=%async_computation.4 | async-start | bytes 9437184 | tf_op jit(solution)/shard_map/all_gather | solution.py:87
  10.4 35.5 %copy-start.73 = (s32[1,1024]{1,0:T(1,128)S(1)}, s32[1,1024]{1,0:T(1,128)}, u32[]{:S(2)}) copy-start(s32[1,1024]{1,0:T(1,128)} %param.21) | copy-start | bytes 12292
  10.4 254.1 %all-gather.8.cloned.1.call-start = ((), (), s32[]{:S(2)}) async-start(), calls=%async_computation.5 | async-start | bytes 9437184 | tf_op jit(solution)/shard_map/all_gather | solution.py:147
  13.2 376.3 %all-gather.10.cloned.1.call-start = ((), (), s32[]{:S(2)}) async-start(), calls=%async_computation.6 | async-start | bytes 9437184 | tf_op jit(solution)/shard_map/all_gather | solution.py:148
  13.3 37.3 %copy-start.32 = (bf16[1024,1024]{1,0:T(8,128)(2,1)S(1)}, bf16[1024,1024]{1,0:T(8,128)(2,1)}, u32[]{:S(2)}) copy-start(bf16[1024,1024]{1,0:T(8,128)(2,1)} %param.20) | copy-start | bytes 6291460
  16.2 716.7 %reduce-scatter.7.cloned.1.call-start = ((), (), s32[]{:S(2)}) async-start(), calls=%async_computation.8 | async-start | bytes 18874368 | tf_op jit(solution)/shard_map/reduce_scatter | solution.py:165
  53.8 147.7 %copy-start.9 = (pred[512,1024]{1,0:T(8,128)(4,1)}, pred[512,1024]{1,0:T(8,128)(4,1)S(1)}, u32[]{:S(2)}) copy-start(pred[512,1024]{1,0:T(8,128)(4,1)S(1)} %get-tuple-element.143) | copy-start | bytes 1572868
  53.8 195.0 %copy-start.11 = (pred[512,1024]{1,0:T(8,128)(4,1)}, pred[512,1024]{1,0:T(8,128)(4,1)S(1)}, u32[]{:S(2)}) copy-start(pred[512,1024]{1,0:T(8,128)(4,1)S(1)} %get-tuple-element.144) | copy-start | bytes 1572868
  158.8 60.2 %copy-start.3 = (bf16[1,1024,1024]{1,2,0:T(8,128)(2,1)}, bf16[1,1024,1024]{1,2,0:T(8,128)(2,1)S(1)}, u32[]{:S(2)}) copy-start(bf16[1,1024,1024]{1,2,0:T(8,128)(2,1)S(1)} %slice.220) | copy-start | bytes 6291460
  159.2 59.7 %copy-start.15 = (bf16[1,1024,16,64]{1,3,2,0:T(8,128)(2,1)}, bf16[1,1024,16,64]{1,3,2,0:T(8,128)(2,1)S(1)}, u32[]{:S(2)}) copy-start(bf16[1,1024,16,64]{1,3,2,0:T(8,128)(2,1)S(1)} %multiply_convert_fusion.5) | copy-start | bytes 6291460
  167.6 33.9 %copy-start.47 = (f32[8,512]{1,0:T(8,128)}, f32[8,512]{1,0:T(8,128)S(1)}, u32[]{:S(2)}) copy-start(f32[8,512]{1,0:T(8,128)S(1)} %get-tuple-element.150) | copy-start | bytes 49156
  181.1 13.5 copy-start.49
  181.1 20.4 %copy-start.59 = (f32[8,512]{1,0:T(8,128)}, f32[8,512]{1,0:T(8,128)S(1)}, u32[]{:S(2)}) copy-start(f32[8,512]{1,0:T(8,128)S(1)} %get-tuple-element.84) | copy-start | bytes 49156
  181.1 13.5 copy-start
  189.2 12.3 copy-start.63
  218.9 29.9 %copy-start.53 = (f32[8,512]{1,0:T(8,128)}, f32[8,512]{1,0:T(8,128)S(1)}, u32[]{:S(2)}) copy-start(f32[8,512]{1,0:T(8,128)S(1)} %get-tuple-element.147) | copy-start | bytes 49156
  219.0 22.0 %copy-start.17 = (bf16[1,1024,16,64]{1,3,2,0:T(8,128)(2,1)S(1)}, bf16[1,1024,16,64]{1,3,2,0:T(8,128)(2,1)}, u32[]{:S(2)}) copy-start(bf16[1,1024,16,64]{1,3,2,0:T(8,128)(2,1)} %add_convert_fusion.2) | copy-start | bytes 6291460
  232.8 16.0 %copy-start.61 = (f32[8,512]{1,0:T(8,128)}, f32[8,512]{1,0:T(8,128)S(1)}, u32[]{:S(2)}) copy-start(f32[8,512]{1,0:T(8,128)S(1)} %get-tuple-element.86) | copy-start | bytes 49156
  232.8 11.0 copy-start.1
  248.8 8.7 copy-start.29
  248.8 8.6 copy-start.37
  248.9 8.6 copy-start.84
  264.6 125.0 %copy-start.83 = (f32[1,1024]{1,0:T(1,128)S(1)}, f32[1,1024]{1,0:T(1,128)}, u32[]{:S(2)}) copy-start(f32[1,1024]{1,0:T(1,128)} %get-tuple-element.134) | copy-start | bytes 12292
  414.6 24.6 %copy-start.6 = (f32[1024,1024]{0,1:T(8,128)S(1)}, f32[1024,1024]{0,1:T(8,128)}, u32[]{:S(2)}) copy-start(f32[1024,1024]{0,1:T(8,128)} %copy-done.5) | copy-start | bytes 12582916
  454.3 561.6 %reduce-scatter.9.cloned.1.call-start = ((), (), s32[]{:S(2)}) async-start(), calls=%async_computation.9 | async-start | bytes 18874368 | tf_op jit(solution)/shard_map/reduce_scatter | solution.py:166
  471.0 20.4 %copy-start.54 = (f32[8,512]{1,0:T(8,128)S(1)}, f32[8,512]{1,0:T(8,128)}, u32[]{:S(2)}) copy-start(f32[8,512]{1,0:T(8,128)} %copy-done.53) | copy-start | bytes 49156
  471.1 20.4 %copy-start.62 = (f32[8,512]{1,0:T(8,128)S(1)}, f32[8,512]{1,0:T(8,128)}, u32[]{:S(2)}) copy-start(f32[8,512]{1,0:T(8,128)} %copy-done.61) | copy-start | bytes 49156
  471.1 21.0 %copy-start.48 = (f32[8,512]{1,0:T(8,128)S(1)}, f32[8,512]{1,0:T(8,128)}, u32[]{:S(2)}) copy-start(f32[8,512]{1,0:T(8,128)} %copy-done.47) | copy-start | bytes 49156
  471.1 21.0 %copy-start.60 = (f32[8,512]{1,0:T(8,128)S(1)}, f32[8,512]{1,0:T(8,128)}, u32[]{:S(2)}) copy-start(f32[8,512]{1,0:T(8,128)} %copy-done.59) | copy-start | bytes 49156
  471.1 21.6 %copy-start.50 = (f32[8,512]{1,0:T(8,128)S(1)}, f32[8,512]{1,0:T(8,128)}, u32[]{:S(2)}) copy-start(f32[8,512]{1,0:T(8,128)} %copy-done.49) | copy-start | bytes 49156
  471.1 21.6 %copy-start.64 = (f32[8,512]{1,0:T(8,128)S(1)}, f32[8,512]{1,0:T(8,128)}, u32[]{:S(2)}) copy-start(f32[8,512]{1,0:T(8,128)} %copy-done.63) | copy-start | bytes 49156
  471.1 22.2 %copy-start.52 = (f32[8,512]{1,0:T(8,128)S(1)}, f32[8,512]{1,0:T(8,128)}, u32[]{:S(2)}) copy-start(f32[8,512]{1,0:T(8,128)} %copy-done.51) | copy-start | bytes 49156
  471.1 22.2 %copy-start.66 = (f32[8,512]{1,0:T(8,128)S(1)}, f32[8,512]{1,0:T(8,128)}, u32[]{:S(2)}) copy-start(f32[8,512]{1,0:T(8,128)} %copy-done.65) | copy-start | bytes 49156
  471.1 827.6 %reduce-scatter.5.cloned.1.call-start = ((), (), s32[]{:S(2)}) async-start(), calls=%async_computation.7 | async-start | bytes 18874368 | tf_op jit(solution)/shard_map/reduce_scatter | solution.py:254
  472.6 21.3 %copy-start.7 = (f32[1024,1024]{0,1:T(8,128)S(1)}, f32[1024,1024]{0,1:T(8,128)}, u32[]{:S(2)}) copy-start(f32[1024,1024]{0,1:T(8,128)} %copy-done.5) | copy-start | bytes 12582916
  501.6 9.1 copy-start.25
  501.6 17.5 %slice-start = ((s8[16777216]{0:T(1024)(128)(4,1)}), s8[4194304]{0:T(1024)(128)(4,1)S(1)}, s32[]{:S(2)}) async-start(s8[16777216]{0:T(1024)(128)(4,1)} %bitcast.262), calls=%async_computation.13 | async-start | bytes 8388608
  501.7 17.5 %slice-start.1 = ((s8[16777216]{0:T(1024)(128)(4,1)}), s8[4194304]{0:T(1024)(128)(4,1)S(1)}, s32[]{:S(2)}) async-start(s8[16777216]{0:T(1024)(128)(4,1)} %bitcast.262), calls=%async_computation.14 | async-start | bytes 8388608
  510.7 8.5 slice-start.3
  510.7 8.5 copy-start.10
  519.2 21.0 %copy-start.12 = (pred[512,1024]{1,0:T(8,128)(4,1)S(1)}, pred[512,1024]{1,0:T(8,128)(4,1)}, u32[]{:S(2)}) copy-start(pred[512,1024]{1,0:T(8,128)(4,1)} %copy-done.11) | copy-start | bytes 1572868
  540.2 25.4 %copy-start.43 = (f32[8,512]{1,0:T(8,128)S(1)}, f32[8,512]{1,0:T(8,128)}, u32[]{:S(2)}) copy-start(f32[8,512]{1,0:T(8,128)} %log_add_fusion.2) | copy-start | bytes 49156
  540.2 25.4 %copy-start.44 = (f32[8,512]{1,0:T(8,128)S(1)}, f32[8,512]{1,0:T(8,128)}, u32[]{:S(2)}) copy-start(f32[8,512]{1,0:T(8,128)} %log_add_fusion.3) | copy-start | bytes 49156
  540.2 25.4 %copy-start.45 = (f32[8,512]{1,0:T(8,128)S(1)}, f32[8,512]{1,0:T(8,128)}, u32[]{:S(2)}) copy-start(f32[8,512]{1,0:T(8,128)} %log_add_fusion.1) | copy-start | bytes 49156
  540.2 25.4 %copy-start.46 = (f32[8,512]{1,0:T(8,128)S(1)}, f32[8,512]{1,0:T(8,128)}, u32[]{:S(2)}) copy-start(f32[8,512]{1,0:T(8,128)} %log_add_fusion) | copy-start | bytes 49156
  540.2 25.4 %copy-start.57 = (f32[8,512]{1,0:T(8,128)S(1)}, f32[8,512]{1,0:T(8,128)}, u32[]{:S(2)}) copy-start(f32[8,512]{1,0:T(8,128)} %get-tuple-element.82) | copy-start | bytes 49156
  540.2 25.4 %copy-start.58 = (f32[8,512]{1,0:T(8,128)S(1)}, f32[8,512]{1,0:T(8,128)}, u32[]{:S(2)}) copy-start(f32[8,512]{1,0:T(8,128)} %get-tuple-element.83) | copy-start | bytes 49156
  618.1 18.6 %copy-start.2 = (bf16[8,512,1024]{2,1,0:T(8,128)(2,1)}, bf16[8,512,1024]{2,1,0:T(8,128)(2,1)S(1)}, u32[]{:S(2)}) copy-start(bf16[8,512,1024]{2,1,0:T(8,128)(2,1)S(1)} %get-tuple-element.127) | copy-start | bytes 25165828
  618.1 9.7 copy-start.4
  618.2 15.9 %slice-start.10 = ((s8[8388608]{0:T(1024)(128)(4,1)}), s8[4194304]{0:T(1024)(128)(4,1)S(1)}, s32[]{:S(2)}) async-start(s8[8388608]{0:T(1024)(128)(4,1)} %bitcast.268), calls=%async_computation.23 | async-start | bytes 8388608
  645.6 10.3 slice-start.12
  674.5 20.2 %slice-start.4 = ((s8[16777216]{0:T(1024)(128)(4,1)}), s8[4194304]{0:T(1024)(128)(4,1)S(1)}, s32[]{:S(2)}) async-start(s8[16777216]{0:T(1024)(128)(4,1)} %bitcast.264), calls=%async_computation.17 | async-start | bytes 8388608
  674.6 20.2 %slice-start.5 = ((s8[16777216]{0:T(1024)(128)(4,1)}), s8[4194304]{0:T(1024)(128)(4,1)S(1)}, s32[]{:S(2)}) async-start(s8[16777216]{0:T(1024)(128)(4,1)} %bitcast.264), calls=%async_computation.18 | async-start | bytes 8388608
  684.1 10.7 slice-start.6
  684.1 10.7 slice-start.7
  727.6 628.2 %reduce-scatter.11.cloned.1.call-start = ((), (), s32[]{:S(2)}) async-start(), calls=%async_computation.10 | async-start | bytes 73728 | tf_op jit(solution)/shard_map/reduce_scatter | solution.py:255
  730.6 285.2 %copy-start.21 = (f32[512,1024]{1,0:T(8,128)S(1)}, f32[512,1024]{1,0:T(8,128)}, u32[]{:S(2)}) copy-start(f32[512,1024]{1,0:T(8,128)} %param.30) | copy-start | bytes 6291460
  730.7 678.6 %all-reduce.3.cloned.1.call-start = ((), (), s32[]{:S(2)}) async-start(), calls=%async_computation.12 | async-start | bytes 4194304 | tf_op jit(solution)/shard_map/psum | solution.py:272
  1023.1 275.6 %copy-start.14 = (f32[4,128,1024]{1,2,0:T(8,128)S(1)}, f32[4,128,1024]{1,2,0:T(8,128)}, u32[]{:S(2)}) copy-start(f32[4,128,1024]{1,2,0:T(8,128)} %copy-done.13) | copy-start | bytes 6291460
  1023.1 422.9 %all-gather.12.cloned.1.call-start = ((), (), s32[]{:S(2)}) async-start(), calls=%async_computation.11 | async-start | bytes 5242880 | tf_op jit(solution)/shard_map/all_gather | solution.py:269
  1322.4 33.5 %copy-start.56 = (f32[12,128]{1,0:T(8,128)S(1)}, f32[12,128]{1,0:T(8,128)}, u32[]{:S(2)}) copy-start(f32[12,128]{1,0:T(8,128)} %param.34) | copy-start | bytes 18436
  1322.4 33.5 %copy-start.79 = (f32[1,12,128]{2,0,1:T(1,128)S(1)}, f32[1,12,128]{2,0,1:T(1,128)}, u32[]{:S(2)}) copy-start(f32[1,12,128]{2,0,1:T(1,128)} %param.36) | copy-start | bytes 18436
  1322.4 33.5 %copy-start.80 = (f32[1,12,128]{2,0,1:T(1,128)S(1)}, f32[1,12,128]{2,0,1:T(1,128)}, u32[]{:S(2)}) copy-start(f32[1,12,128]{2,0,1:T(1,128)} %param.37) | copy-start | bytes 18436
  1322.4 41.3 %copy-start.78 = (f32[12,128]{1,0:T(8,128)S(1)}, f32[12,128]{1,0:T(8,128)}, u32[]{:S(2)}) copy-start(f32[12,128]{1,0:T(8,128)} %param.35) | copy-start | bytes 18436
  (44 other events, 169.5 us)
Sparse Core Ops, SparseCore 0:
  10.6 128.0 all-gather.5
  141.4 122.6 all-gather.7
  266.8 122.6 all-gather.9
  454.4 278.3 reduce-scatter.6
  736.5 279.3 reduce-scatter.8
  1019.5 279.2 reduce-scatter.4
  1301.9 53.9 reduce-scatter.10
  1358.8 50.4 all-reduce.2
  1411.4 34.5 all-gather.11
